TPU v7x, 32 devices: a whole 2x2x4 slice. The times are simulated.
32 devices in a mesh: parts: 2 (over x), dp: 16 (over z, y, core).
Axes of the slice: x: 2, y: 2, z: 4, core: 2. Of those that a mesh axis runs over, the one named last changes fastest.
Arguments:
- activations: bfloat16 [8192, 14336], P(('parts', 'dp')), parts along dimension 0, may hold values from -6 to 6
- out_grads: bfloat16 [8192, 4096], P(('parts', 'dp')), parts along dimension 0, may hold values from -6 to 6
- lengths: int32 [32, 4], P(('parts', 'dp')), parts along dimension 0, may hold values from 1 to 128, 256 in all within a row
- proj_in: bfloat16 [14336, 64], replicated, may hold values from -0.046875 to 0.046875
- proj_out: bfloat16 [4096, 64], replicated, may hold values from -0.09375 to 0.09375
- queries: bfloat16 [1024, 4096], P(('parts', 'dp')), parts along dimension 0, may hold values from -0.01171875 to 0.01171875
Outputs:
- scores: bfloat16 [128, 512], P(('parts', 'dp')), parts along dimension 0
There are 2 independent parts, one for each index of `parts`. A program takes and returns all parts, laid end to end along the dimension named above; an argument that names none is the same for every part. Nothing has to cross between parts.
Inputs may be any that keep to these rules, and one draw needn't show every extreme that they name: Each row of lengths sums to 256, and one entry of each row equals 128.
All inputs are finite; a program needn't handle non-finite values.
Results may differ from a plain program's by a relative error of at most 0.0065.
Values may be sent and summed in bfloat16 or wider, within the bound.
A program may use at most 128 MiB of HBM per device.

v0:
```python
import jax
import jax.numpy as jnp
from jax import lax
from jax.sharding import PartitionSpec as P


def local(activations, out_grads, lengths, proj_in, proj_out, queries):
    tok_count = activations.shape[0]
    rank_size = proj_in.shape[1]
    proj_acts = jnp.dot(activations, proj_in, preferred_element_type=jnp.float32).astype(
        jnp.bfloat16
    )
    proj_grads = jnp.dot(out_grads, proj_out, preferred_element_type=jnp.float32).astype(
        jnp.bfloat16
    )
    counts = lengths[0]
    tok_ends = jnp.cumsum(counts)
    tok_starts = tok_ends - counts
    position = jnp.arange(tok_count, dtype=jnp.int32)
    member = (
        (position[None, :] >= tok_starts[:, None]) & (position[None, :] < tok_ends[:, None])
    ).astype(jnp.bfloat16)
    masked_grads = member[:, :, None] * proj_grads[None, :, :]
    summed = jnp.einsum("eti,tj->eij", masked_grads, proj_acts, preferred_element_type=jnp.float32)
    example_grads = summed.reshape(counts.shape[0], rank_size * rank_size).astype(jnp.bfloat16)
    contract = (((1,), (1,)), ((), ()))
    local_scores = lax.dot_general(
        lax.all_gather(example_grads, "dp", axis=0, tiled=True),
        queries,
        contract,
        preferred_element_type=jnp.float32,
    ).astype(jnp.bfloat16)
    return lax.all_to_all(local_scores, "dp", split_axis=0, concat_axis=1, tiled=True)


def solution(mesh):
    in_specs = (
        P(("parts", "dp"), None),
        P(("parts", "dp"), None),
        P(("parts", "dp"), None),
        P(),
        P(),
        P(("parts", "dp"), None),
    )
    out_specs = P(("parts", "dp"), None)
    return jax.shard_map(local, mesh=mesh, in_specs=in_specs, out_specs=out_specs, check_vma=False)
```

profile of v0, /device:TPU:0, one launch (start us, length us, event | category | flops | bytes accessed | tf_op | source)
XLA Modules:
  0.0 44.8 jit_solution(8421804942782179360)
XLA Ops:
  0.0 0.0 copy-start
  0.0 1.0 %reduce-window.7 = s32[4,1]{0,1:T(1,128)S(1)} reduce-window(s32[4,1]{0,1:T(1,128)} %bitcast.20, s32[]{:T(128)} %constant.3.clone.1), window={size=4x1 pad=3_0x0_0}, to_apply=%region_0.0 | reduce-window | flops 12 | bytes 36 | tf_op jit(solution)/shard_map/reduce-window.2
  1.0 0.7 %bitcast_subtract_fusion = s32[4]{0:T(128)S(1)} fusion(s32[1,4]{1,0:T(1,128)} %param.8, s32[4,1]{0,1:T(1,128)S(1)} %reduce-window.7), kind=kLoop, calls=%fused_computation.12 | loop fusion | flops 4 | bytes 48 | tf_op jit(solution)/shard_map/sub | solution.py:18
  1.6 0.1 fusion.5
  1.7 0.0 copy-done
  1.7 1.8 %convolution_convert_fusion.2 = bf16[256,64]{0,1:T(8,128)(2,1)S(1)} fusion(bf16[256,4096]{1,0:T(8,128)(2,1)S(1)} %copy-done, bf16[4096,64]{0,1:T(8,128)(2,1)} %param.10), kind=kOutput, calls=%fused_computation.2 | convolution fusion | flops 134234112 | bytes 2654208 | tf_op jit(solution)/shard_map/dot_general | solution.py:13
  3.5 0.0 copy-start.1
  3.5 6.2 %convolution_convert_fusion = bf16[4,64,64]{2,1,0:T(8,128)(2,1)S(1)} fusion(bf16[256,14336]{1,0:T(8,128)(2,1)} %param.6, bf16[14336,64]{0,1:T(8,128)(2,1)} %param.9, bf16[256,64]{0,1:T(8,128)(2,1)S(1)} %convolution_convert_fusion.2, bf16[4,256]{1,0:T(4,128)(2,1)S(1)} %fusion.5), kind=kOutput, calls=%fused_computation | convolution fusion | flops 478248960 | bytes 9242624 | tf_op jit(solution)/shard_map/eti,tj->eij/dot_general | solution.py:24
  9.7 0.1 reshape.80
  9.9 24.6 %all-gather = bf16[16,4,4096]{2,1,0:T(4,128)(2,1)S(1)} all-gather(bf16[1,4,4096]{2,1,0:T(4,128)(2,1)S(1)} %reshape.80), channel_id=1, replica_groups=mesh['parts'=2,'dp'=16] {'dp'}, dimensions={0}, use_global_device_ids=true | all-gather | bytes 557056 | tf_op jit(solution)/shard_map/all_gather | solution.py:28
  34.5 0.1 reshape.81
  34.6 0.0 copy-done.1
  34.6 0.3 convolution_convert_fusion.3
  34.9 0.1 copy.11
  35.0 9.1 %all_to_all.19 = bf16[16,4,32]{2,1,0:T(4,128)(2,1)S(1)} all-to-all(bf16[16,4,32]{2,1,0:T(4,128)(2,1)S(1)} %bitcast.17), channel_id=1, replica_groups=mesh['parts'=2,'dp'=16] {'dp'}, dimensions={0} | all-to-all | bytes 8192 | tf_op jit(solution)/shard_map/all_to_all | solution.py:33
  44.1 0.7 %all_to_all.17 = bf16[4,512]{1,0:T(4,128)(2,1)} reshape(bf16[4,16,32]{2,1,0:T(8,128)(2,1)S(1)} %copy.12) | data formatting | bytes 8192 | tf_op jit(solution)/shard_map/all_to_all | solution.py:33
  (1 shorter events, 0.0 us)
Async XLA Ops:
  0.0 1.7 %copy-start = (bf16[256,4096]{1,0:T(8,128)(2,1)S(1)}, bf16[256,4096]{1,0:T(8,128)(2,1)}, u32[]{:S(2)}) copy-start(bf16[256,4096]{1,0:T(8,128)(2,1)} %param.7) | copy-start | bytes 6291460
  3.5 31.1 %copy-start.1 = (bf16[32,4096]{1,0:T(8,128)(2,1)S(1)}, bf16[32,4096]{1,0:T(8,128)(2,1)}, u32[]{:S(2)}) copy-start(bf16[32,4096]{1,0:T(8,128)(2,1)} %param.11) | copy-start | bytes 786436
where the time goes:
time: 45 us; the launch traced here: 44.8 us
  blocking collectives  33.7 us (75%)
  matrix products  8.27 us (18%)
  other arithmetic  1.71 us (4%)
  local copies, waits for them, and re-layouts  1.04 us (2%)
    all_gather x1, blocking collectives, local(): lax.all_gather(example_grads, 'dp', axis=0, tiled=True)  24.6 us
    all_to_all x1, blocking collectives, local(): lax.all_to_all(local_scores, 'dp', split_axis=0, concat_axis=1, tiled=True)  9.07 us
    dot_general x1, matrix products, local(): jnp.einsum('eti,tj->eij', masked_grads, proj_acts, preferred_element_type...  6.21 us
    dot_general x1, matrix products, local(): jnp.dot(out_grads, proj_out, preferred_element_type=jnp.float32)  1.8 us
    another operation x1, other arithmetic  0.97 us

commit v1 on v0

--- a/solution.py
+++ b/solution.py
@@ -2,6 +2,11 @@
 import jax.numpy as jnp
 from jax import lax
 from jax.sharding import PartitionSpec as P
+from jax.lax import all_to_all, axis_size
+
+_handle_sites = lambda xin: jnp.concatenate(
+    all_to_all(jnp.stack(jnp.split(xin, axis_size("dp"), 0), axis=0), "dp", 0, 0), 1
+)
 
 
 def local(activations, out_grads, lengths, proj_in, proj_out, queries):
@@ -30,7 +35,7 @@
         contract,
         preferred_element_type=jnp.float32,
     ).astype(jnp.bfloat16)
-    return lax.all_to_all(local_scores, "dp", split_axis=0, concat_axis=1, tiled=True)
+    return _handle_sites(local_scores)
 
 
 def solution(mesh):

time: 45 us -> 46.7 us (1.038)
  local copies, waits for them, and re-layouts: 1.04 us -> 2.68 us
    split x0 -> x17, local copies, waits for them, and re-layouts: none -> 1.61 us  [jnp.split(xin, axis_size('dp'), 0)]
    all_to_all x2 -> x0, local copies, waits for them, and re-layouts: 0.69 us -> none  [local(): lax.all_to_all(local_scores, 'dp', split_axis=0, concat_axis=1, tiled=True)]
    reshape x0 -> x2, local copies, waits for them, and re-layouts: none -> 0.69 us  [jnp.concatenate(all_to_all(jnp.stack(jnp.split(xin, axis_size('dp'), 0),...]
where the time goes in v1:
time: 46.7 us; the launch traced here: 46.5 us
  blocking collectives  33.7 us (72%)
  matrix products  8.27 us (18%)
  local copies, waits for them, and re-layouts  2.68 us (6%)
  other arithmetic  1.71 us (4%)
    all_gather x1, blocking collectives, local(): lax.all_gather(example_grads, 'dp', axis=0, tiled=True)  24.6 us
    all_to_all x1, blocking collectives, all_to_all(jnp.stack(jnp.split(xin, axis_size('dp'), 0), axis=0), 'dp', 0...  9.07 us
    dot_general x1, matrix products, local(): jnp.einsum('eti,tj->eij', masked_grads, proj_acts, preferred_element_type...  6.21 us
    dot_general x1, matrix products, local(): jnp.dot(out_grads, proj_out, preferred_element_type=jnp.float32)  1.8 us
    split x17, local copies, waits for them, and re-layouts, jnp.split(xin, axis_size('dp'), 0)  1.61 us
    another operation x1, other arithmetic  0.97 us

profile of v1, /device:TPU:0, one launch (start us, length us, event | category | flops | bytes accessed | tf_op | source)
XLA Modules:
  0.0 46.5 jit_solution(14258477820824780418)
XLA Ops:
  0.0 0.0 copy-start
  0.0 1.0 %reduce-window.7 = s32[4,1]{0,1:T(1,128)S(1)} reduce-window(s32[4,1]{0,1:T(1,128)} %bitcast.50, s32[]{:T(128)} %constant.3.clone.1), window={size=4x1 pad=3_0x0_0}, to_apply=%region_0.0 | reduce-window | flops 12 | bytes 36 | tf_op jit(solution)/shard_map/reduce-window.2
  1.0 0.7 %bitcast_subtract_fusion = s32[4]{0:T(128)S(1)} fusion(s32[1,4]{1,0:T(1,128)} %param.8, s32[4,1]{0,1:T(1,128)S(1)} %reduce-window.7), kind=kLoop, calls=%fused_computation.28 | loop fusion | flops 4 | bytes 48 | tf_op jit(solution)/shard_map/sub | solution.py:23
  1.6 0.1 fusion.5
  1.7 0.0 copy-done
  1.7 1.8 %convolution_convert_fusion.2 = bf16[256,64]{0,1:T(8,128)(2,1)S(1)} fusion(bf16[256,4096]{1,0:T(8,128)(2,1)S(1)} %copy-done, bf16[4096,64]{0,1:T(8,128)(2,1)} %param.10), kind=kOutput, calls=%fused_computation.2 | convolution fusion | flops 134234112 | bytes 2654208 | tf_op jit(solution)/shard_map/dot_general | solution.py:18
  3.5 0.0 copy-start.1
  3.5 6.2 %convolution_convert_fusion = bf16[4,64,64]{2,1,0:T(8,128)(2,1)S(1)} fusion(bf16[256,14336]{1,0:T(8,128)(2,1)} %param.6, bf16[14336,64]{0,1:T(8,128)(2,1)} %param.9, bf16[256,64]{0,1:T(8,128)(2,1)S(1)} %convolution_convert_fusion.2, bf16[4,256]{1,0:T(4,128)(2,1)S(1)} %fusion.5), kind=kOutput, calls=%fused_computation | convolution fusion | flops 478248960 | bytes 9242624 | tf_op jit(solution)/shard_map/eti,tj->eij/dot_general | solution.py:29
  9.7 0.1 reshape.85
  9.9 24.6 %all-gather = bf16[16,4,4096]{2,1,0:T(4,128)(2,1)S(1)} all-gather(bf16[1,4,4096]{2,1,0:T(4,128)(2,1)S(1)} %reshape.85), channel_id=1, replica_groups=mesh['parts'=2,'dp'=16] {'dp'}, dimensions={0}, use_global_device_ids=true | all-gather | bytes 557056 | tf_op jit(solution)/shard_map/all_gather | solution.py:33
  34.5 0.1 reshape.86
  34.6 0.0 copy-done.1
  34.6 0.3 convolution_convert_fusion.3
  34.9 0.1 fusion.6
  35.0 0.1 copy.55
  35.1 0.1 copy.54
  35.2 0.1 copy.53
  35.3 0.1 copy.52
  35.4 0.1 copy.51
  35.5 0.1 copy.50
  35.5 0.1 copy.49
  35.6 0.1 copy.48
  35.7 0.1 copy.47
  35.8 0.1 copy.46
  35.9 0.1 copy.45
  36.0 0.1 copy.44
  36.1 0.1 copy.43
  36.2 0.1 copy.42
  36.3 0.1 copy.41
  36.4 0.1 copy.40
  36.7 9.1 %all_to_all.5 = bf16[16,4,32]{2,1,0:T(4,128)(2,1)S(1)} all-to-all(bf16[16,4,32]{2,1,0:T(4,128)(2,1)S(1)} %constant_dynamic-update-slice_fusion), channel_id=1, replica_groups=mesh['parts'=2,'dp'=16] {'dp'}, dimensions={0} | all-to-all | bytes 8192 | tf_op jit(solution)/shard_map/all_to_all | solution.py:8
  45.8 0.7 %reshape.84 = bf16[4,512]{1,0:T(4,128)(2,1)} reshape(bf16[4,16,32]{2,1,0:T(8,128)(2,1)S(1)} %copy.56) | data formatting | bytes 8192 | tf_op jit(solution)/shard_map/reshape | solution.py:7
  (17 shorter events, 0.1 us)
Async XLA Ops:
  0.0 1.7 %copy-start = (bf16[256,4096]{1,0:T(8,128)(2,1)S(1)}, bf16[256,4096]{1,0:T(8,128)(2,1)}, u32[]{:S(2)}) copy-start(bf16[256,4096]{1,0:T(8,128)(2,1)} %param.7) | copy-start | bytes 6291460
  3.5 31.1 %copy-start.1 = (bf16[32,4096]{1,0:T(8,128)(2,1)S(1)}, bf16[32,4096]{1,0:T(8,128)(2,1)}, u32[]{:S(2)}) copy-start(bf16[32,4096]{1,0:T(8,128)(2,1)} %param.11) | copy-start | bytes 786436
